TPU v7x, 32 devices: a whole 2x2x4 slice. The times are simulated.
32 devices in a mesh: wide: 8 (over z, x), group: 4 (over y, core).
Axes of the slice: x: 2, y: 2, z: 4, core: 2. Of those that a mesh axis runs over, the one named last changes fastest.
Arguments:
- feat4: bfloat16 [32, 24, 24, 256], P(('wide', 'group')), may hold values from -100 to 100
- feat5: bfloat16 [32, 12, 12, 256], P(('wide', 'group')), may hold values from -100 to 100
- feat6: bfloat16 [32, 6, 6, 256], P(('wide', 'group')), may hold values from -100 to 100
- feat7: bfloat16 [32, 3, 3, 256], P(('wide', 'group')), may hold values from -100 to 100
- out_grad4: bfloat16 [32, 24, 24, 256], P(('wide', 'group')), may hold values from -6 to 6
- out_grad5: bfloat16 [32, 12, 12, 256], P(('wide', 'group')), may hold values from -6 to 6
- out_grad6: bfloat16 [32, 6, 6, 256], P(('wide', 'group')), may hold values from -6 to 6
- out_grad7: bfloat16 [32, 3, 3, 256], P(('wide', 'group')), may hold values from -6 to 6
- conv_weight: bfloat16 [3, 3, 256, 256], replicated, may hold values from -0.125 to 0.125
- bn_gain: float32 [4, 256], replicated, may hold values from 0.25 to 1.75
- bn_shift: float32 [4, 256], replicated, may hold values from -0.5 to 0.5
- heights: int32 [32], P(('wide', 'group')), may hold values from 168 to 384
- widths: int32 [32], P(('wide', 'group')), may hold values from 168 to 384
Outputs:
- out4: bfloat16 [32, 24, 24, 256], P(('wide', 'group'))
- out5: bfloat16 [32, 12, 12, 256], P(('wide', 'group'))
- out6: bfloat16 [32, 6, 6, 256], P(('wide', 'group'))
- out7: bfloat16 [32, 3, 3, 256], P(('wide', 'group'))
- d_feat4: bfloat16 [32, 24, 24, 256], P(('wide', 'group'))
- d_feat5: bfloat16 [32, 12, 12, 256], P(('wide', 'group'))
- d_feat6: bfloat16 [32, 6, 6, 256], P(('wide', 'group'))
- d_feat7: bfloat16 [32, 3, 3, 256], P(('wide', 'group'))
- d_weight: float32 [3, 3, 256, 256], replicated
- d_gain: float32 [4, 256], replicated
- d_shift: float32 [4, 256], replicated
Inputs may be any that keep to these rules, and one draw needn't show every extreme that they name: `heights`: pixel height of the valid part of each image. `widths`: pixel width of the valid part of each image.
All inputs are finite; a program needn't handle non-finite values.
Results may differ from a plain program's by a relative error of at most 0.0049.
Values sent between devices are 32-bit elements; how exact they have to be, the bound alone decides.
No kernel may reach another device: no remote copies, remote signals or barrier semaphores. Data moves between devices by JAX's collectives and lax.ppermute only.
A program may use at most 64 MiB of HBM per device.

v0:
```python
import jax
import jax.numpy as jnp
from jax import lax
from jax.sharding import PartitionSpec as P

EPSILON = 1e-05


def level_mask(heights, widths, stride, extent):
    row_limit = (heights[0] + stride - 1) // stride
    col_limit = (widths[0] + stride - 1) // stride
    row_place = lax.broadcasted_iota(jnp.int32, (extent, extent), 0)
    col_place = lax.broadcasted_iota(jnp.int32, (extent, extent), 1)
    inside = jnp.logical_and(row_place < row_limit, col_place < col_limit)
    return (inside.astype(jnp.float32), row_limit)


def conv_rows(padded, conv_weight, start_row, row_count, extent):
    summed = jnp.zeros((row_count * extent, conv_weight.shape[3]), jnp.float32)
    for tap_row in range(3):
        for tap_col in range(3):
            window = lax.dynamic_slice_in_dim(padded, start_row + tap_row, row_count, 0)[
                :, tap_col : tap_col + extent, :
            ]
            summed = summed + jnp.dot(
                window.reshape(row_count * extent, -1),
                conv_weight[tap_row, tap_col],
                preferred_element_type=jnp.float32,
            )
    return summed.reshape(row_count, extent, -1)


def input_grad_rows(padded_back, conv_weight, start_row, row_count, extent):
    summed = jnp.zeros((row_count * extent, conv_weight.shape[2]), jnp.float32)
    for tap_row in range(3):
        for tap_col in range(3):
            window = lax.dynamic_slice_in_dim(padded_back, start_row + 2 - tap_row, row_count, 0)[
                :, 2 - tap_col : 2 - tap_col + extent, :
            ]
            summed = summed + lax.dot_general(
                window.reshape(row_count * extent, -1),
                conv_weight[tap_row, tap_col],
                (((1,), (1,)), ((), ())),
                preferred_element_type=jnp.float32,
            )
    return summed.reshape(row_count, extent, -1)


def weight_grad_rows(padded, back_rows, start_row, row_count, extent):
    flat_back = back_rows.reshape(row_count * extent, -1)
    tap_terms = []
    for tap_row in range(3):
        for tap_col in range(3):
            window = lax.dynamic_slice_in_dim(padded, start_row + tap_row, row_count, 0)[
                :, tap_col : tap_col + extent, :
            ]
            tap_terms.append(
                lax.dot_general(
                    window.reshape(row_count * extent, -1),
                    flat_back,
                    (((0,), (0,)), ((), ())),
                    preferred_element_type=jnp.float32,
                )
            )
    return jnp.stack(tap_terms).reshape(3, 3, padded.shape[2], flat_back.shape[1])


def forward_conv(padded, conv_weight, extent):
    conv_out = conv_rows(padded, conv_weight, 0, extent, extent)
    return conv_out


def backward_conv(padded, back_grad, conv_weight, extent):
    padded_back = jnp.pad(back_grad, ((1, 1), (1, 1), (0, 0)))
    weight_part = weight_grad_rows(padded, back_grad, 0, extent, extent)
    input_part = input_grad_rows(padded_back, conv_weight, 0, extent, extent)
    return (weight_part, input_part)


def combine_stats(values):
    within = lax.psum(values, "group")
    result = lax.psum(within, "wide")
    return result


def combine_grads(values):
    within = lax.psum(values, "group")
    result = lax.psum(within, "wide")
    return result


def shards(
    feat4,
    feat5,
    feat6,
    feat7,
    out_grad4,
    out_grad5,
    out_grad6,
    out_grad7,
    conv_weight,
    bn_gain,
    bn_shift,
    heights,
    widths,
):
    features = (feat4, feat5, feat6, feat7)
    cotangents = (out_grad4, out_grad5, out_grad6, out_grad7)
    devices = lax.axis_size("wide") * lax.axis_size("group")
    levels = []
    for level_index in range(4):
        feature = features[level_index][0]
        extent = feature.shape[0]
        valid_mask, row_limit = level_mask(heights, widths, 16 * 2**level_index, extent)
        weighted = valid_mask[:, :, None]
        padded = jnp.pad(feature * weighted.astype(feature.dtype), ((1, 1), (1, 1), (0, 0)))
        conv_out = forward_conv(padded, conv_weight, extent)
        levels.append((valid_mask, row_limit, weighted, padded, conv_out))
    moments = []
    local_sums = jnp.stack(
        [jnp.sum(level_entry[4] * level_entry[2], axis=(0, 1)) for level_entry in levels]
    )
    local_squares = jnp.stack(
        [
            jnp.sum(level_entry[2] * level_entry[4] * level_entry[4], axis=(0, 1))
            for level_entry in levels
        ]
    )
    local_counts = jnp.stack([jnp.sum(level_entry[0]) for level_entry in levels])
    moment_sums, squares, counts = combine_stats((local_sums, local_squares, local_counts))
    for level_index in range(4):
        pixel_count = counts[level_index]
        mean_value = moment_sums[level_index] / pixel_count
        moments.append(
            (pixel_count, mean_value, squares[level_index] / pixel_count - mean_value * mean_value)
        )
    finals = []
    for level_index in range(4):
        valid_mask, row_limit, weighted, padded, conv_out = levels[level_index]
        pixel_count, mean_value, variance = moments[level_index]
        inverse = lax.rsqrt(variance + EPSILON)
        normed = (conv_out - mean_value) * inverse
        shifted = bn_gain[level_index] * normed + bn_shift[level_index]
        sigmoid_value = jax.nn.sigmoid(shifted)
        output = (weighted * shifted * sigmoid_value).astype(jnp.bfloat16)
        slope_term = (
            weighted
            * cotangents[level_index][0].astype(jnp.float32)
            * sigmoid_value
            * (1.0 + shifted * (1.0 - sigmoid_value))
        )
        finals.append((output, normed, inverse, slope_term))
    shift_local = jnp.stack([jnp.sum(final_entry[3], axis=(0, 1)) for final_entry in finals])
    gain_local = jnp.stack(
        [jnp.sum(final_entry[3] * final_entry[1], axis=(0, 1)) for final_entry in finals]
    )
    shift_rows, gain_rows = combine_stats((shift_local, gain_local))
    back_sums = [(shift_rows[level_index], gain_rows[level_index]) for level_index in range(4)]
    weight_local = jnp.zeros(conv_weight.shape, jnp.float32)
    outputs = []
    input_grads = []
    shift_list = []
    gain_list = []
    for level_index in range(4):
        valid_mask, row_limit, weighted, padded, conv_out = levels[level_index]
        pixel_count, mean_value, variance = moments[level_index]
        output, normed, inverse, slope_term = finals[level_index]
        shift_sum, gain_sum = back_sums[level_index]
        extent = conv_out.shape[0]
        back_grad = (
            weighted
            * (bn_gain[level_index] * inverse)
            * (slope_term - shift_sum / pixel_count - normed * (gain_sum / pixel_count))
        ).astype(jnp.bfloat16)
        weight_part, input_part = backward_conv(padded, back_grad, conv_weight, extent)
        weight_local = weight_local + weight_part
        input_grads.append((weighted * input_part).astype(jnp.bfloat16)[None])
        outputs.append(output[None])
        shift_list.append(shift_sum)
        gain_list.append(gain_sum)
    weight_total = combine_grads(weight_local)
    return (
        outputs[0],
        outputs[1],
        outputs[2],
        outputs[3],
        input_grads[0],
        input_grads[1],
        input_grads[2],
        input_grads[3],
        weight_total / devices,
        jnp.stack(gain_list) / devices,
        jnp.stack(shift_list) / devices,
    )


def solution(mesh):
    placed = (
        P(("wide", "group"), None, None, None),
        P(("wide", "group"), None, None, None),
        P(("wide", "group"), None, None, None),
        P(("wide", "group"), None, None, None),
        P(("wide", "group"), None, None, None),
        P(("wide", "group"), None, None, None),
        P(("wide", "group"), None, None, None),
        P(("wide", "group"), None, None, None),
        P(),
        P(),
        P(),
        P(("wide", "group")),
        P(("wide", "group")),
    )
    return jax.shard_map(
        shards,
        mesh=mesh,
        in_specs=placed,
        out_specs=(
            P(("wide", "group"), None, None, None),
            P(("wide", "group"), None, None, None),
            P(("wide", "group"), None, None, None),
            P(("wide", "group"), None, None, None),
            P(("wide", "group"), None, None, None),
            P(("wide", "group"), None, None, None),
            P(("wide", "group"), None, None, None),
            P(("wide", "group"), None, None, None),
            P(),
            P(),
            P(),
        ),
        check_vma=False,
    )
```

profile of v0, /device:TPU:0, one launch (start us, length us, event | category | flops | bytes accessed | tf_op | source)
XLA Modules:
  0.0 299.1 jit_solution(16657673691624110499)
XLA Ops:
  8.7 0.7 fusion.283
  9.4 0.7 and_convert_fusion.9
  10.1 0.7 fusion.281
  10.8 0.7 and_convert_fusion.3
  11.5 0.8 bitcast_multiply_fusion.8
  12.2 0.8 broadcast_multiply_fusion.4
  13.0 0.6 fusion.268
  13.8 0.7 fusion.257
  14.5 0.7 and_convert_fusion
  15.2 0.8 bitcast_multiply_fusion.6
  16.0 0.8 broadcast_multiply_fusion.3
  17.4 1.0 fusion.131
  18.4 1.1 convolution_add_fusion.63
  19.4 1.1 convolution_add_fusion.62
  21.9 0.7 multiply_reduce_fusion.6
  22.6 0.6 reshape.1117
  26.4 0.7 multiply_reduce_fusion.4
  27.2 0.6 reshape.1116
  31.1 0.7 reshape.1115
  35.5 2.6 pad_maximum_fusion.4
  38.2 8.7 %all-reduce.11 = (f32[4,256]{1,0:T(4,128)S(1)}, f32[4]{0:T(128)S(1)}, f32[4,256]{1,0:T(4,128)S(1)}) all-reduce(f32[4,256]{1,0:T(4,128)S(1)} %pad_maximum_fusion.1, f32[4]{0:T(128)S(1)} %pad_maximum_fusion.4, f32[4,256]{1,0:T(4,128)S(1)} %pad_maximum_fusion), channel_id=1, replica_groups=mesh['wide'=8,'group'=4] {'group'}, use_global_device_ids=true, to_apply=%region_16.17 | all-reduce | flops 2052 | bytes 16416 | tf_op jit(solution)/shard_map/psum | solution.py:81
  46.9 22.2 %all-reduce.9 = (f32[4,256]{1,0:T(4,128)S(1)}, f32[4]{0:T(128)S(1)}, f32[4,256]{1,0:T(4,128)S(1)}) all-reduce(f32[4,256]{1,0:T(4,128)S(1)} %get-tuple-element.34, f32[4]{0:T(128)S(1)} %get-tuple-element.35, f32[4,256]{1,0:T(4,128)S(1)} %get-tuple-element.36), channel_id=1, replica_groups=mesh['wide'=8,'group'=4] {'wide'}, use_global_device_ids=true, to_apply=%region_17.18 | all-reduce | flops 2052 | bytes 16416 | tf_op jit(solution)/shard_map/psum | solution.py:82
  69.7 2.6 slice_divide_fusion.8
  72.3 2.6 slice_divide_fusion.9
  78.2 0.7 fusion.299
  78.9 5.9 %all-reduce.10 = (f32[4,256]{1,0:T(4,128)S(1)}, f32[4,256]{1,0:T(4,128)S(1)}) all-reduce(f32[4,256]{1,0:T(4,128)S(1)} %pad_maximum_fusion.3, f32[4,256]{1,0:T(4,128)S(1)} %pad_maximum_fusion.2), channel_id=1, replica_groups=mesh['wide'=8,'group'=4] {'group'}, use_global_device_ids=true, to_apply=%region_28.29 | all-reduce | flops 2048 | bytes 16384 | tf_op jit(solution)/shard_map/psum | solution.py:81
  84.8 17.6 %all-reduce.8 = (f32[4,256]{1,0:T(4,128)S(1)}, f32[4,256]{1,0:T(4,128)S(1)}) all-reduce(f32[4,256]{1,0:T(4,128)S(1)} %get-tuple-element.32, f32[4,256]{1,0:T(4,128)S(1)} %get-tuple-element.33), channel_id=1, replica_groups=mesh['wide'=8,'group'=4] {'wide'}, use_global_device_ids=true, to_apply=%region_29.30 | all-reduce | flops 2048 | bytes 16384 | tf_op jit(solution)/shard_map/psum | solution.py:82
  102.4 2.6 slice_divide_fusion
  105.1 2.6 slice_divide_fusion.1
  107.9 1.1 multiply_convert_fusion.2
  110.7 0.6 fusion.4
  120.9 2.1 add_add_fusion
  123.7 0.6 reshape.1164
  124.3 0.7 reshape.1163
  125.6 0.6 pad_slice_fusion.32
  126.2 0.6 pad_slice_fusion.48
  127.0 1.3 reshape.1156
  128.3 1.3 reshape.1150
  129.6 1.3 reshape.1151
  130.9 1.3 reshape.1152
  132.2 1.3 reshape.1153
  133.5 0.7 reshape.1154
  135.0 0.9 convolution_add_fusion.55
  135.9 0.9 convolution_add_fusion.54
  136.8 0.9 convolution_add_fusion.53
  137.6 1.0 convolution_add_fusion.52
  138.6 0.9 convolution_add_fusion.51
  140.1 1.4 multiply_convert_fusion.21
  141.5 0.6 reshape.1141
  142.1 0.6 reshape.1142
  142.7 0.6 reshape.1143
  145.3 0.9 convolution_add_fusion.39
  146.2 0.9 convolution_add_fusion.38
  147.1 0.9 convolution_add_fusion.37
  148.1 1.0 convolution_add_fusion.36
  152.4 0.7 reshape.1139
  153.2 1.2 pad_slice_fusion
  154.4 0.7 multiply_convert_fusion.13
  156.1 20.6 %all-reduce.15.cloned.1.call-done = f32[3,3,256,256]{3,2,1,0:T(8,128)} async-done(((f32[3,3,256,256]{3,2,1,0:T(8,128)}), f32[3,3,256,256]{3,2,1,0:T(8,128)}) %all-reduce.15.cloned.1.call-update) | async-done | bytes 2359312 | tf_op jit(solution)/shard_map/psum | solution.py:87
  176.7 1.9 multiply_convert_fusion.6
  179.4 0.7 copy-done.4
  181.7 1.1 multiply_convert_fusion.1
  182.7 106.2 %all-reduce.17.cloned.1.call-done = f32[3,3,256,256]{3,2,1,0:T(8,128)} async-done(((f32[3,3,256,256]{3,2,1,0:T(8,128)}), f32[3,3,256,256]{3,2,1,0:T(8,128)}) %all-reduce.17.cloned.1.call-update) | async-done | bytes 2359312 | tf_op jit(solution)/shard_map/psum | solution.py:88
  289.0 3.3 %broadcast_multiply_fusion = f32[3,3,256,256]{3,2,1,0:T(8,128)} fusion(f32[3,3,256,256]{3,2,1,0:T(8,128)} %all-reduce.17.cloned.1.call-done), kind=kLoop, calls=%fused_computation.17 | loop fusion | flops 589824 | bytes 4718592 | tf_op jit(solution)/shard_map/div | solution.py:191
  (460 shorter events, 37.0 us)
Async XLA Ops:
  7.2 13.3 %copy-start = (bf16[3,3,256,256]{3,2,1,0:T(8,128)(2,1)S(1)}, bf16[3,3,256,256]{3,2,1,0:T(8,128)(2,1)}, u32[]{:S(2)}) copy-start(bf16[3,3,256,256]{3,2,1,0:T(8,128)(2,1)} %param.21) | copy-start | bytes 3538948
  7.2 16.6 %copy-start.9 = (bf16[1,12,12,256]{3,2,1,0:T(8,128)(2,1)S(1)}, bf16[1,12,12,256]{3,2,1,0:T(8,128)(2,1)}, u32[]{:S(2)}) copy-start(bf16[1,12,12,256]{3,2,1,0:T(8,128)(2,1)} %param.14) | copy-start | bytes 221188
  7.2 169.5 %all-reduce.15.cloned.1.call-start = ((), (), s32[]{:S(2)}) async-start(), calls=%async_computation | async-start | bytes 4718592 | tf_op jit(solution)/shard_map/psum | solution.py:87
  13.0 4.1 %copy-start.76 = (bf16[1,3,3,256]{3,2,1,0:T(4,128)(2,1)}, bf16[1,3,3,256]{3,2,1,0:T(4,128)(2,1)S(1)}, u32[]{:S(2)}) copy-start(bf16[1,3,3,256]{3,2,1,0:T(4,128)(2,1)S(1)} %broadcast_multiply_fusion.4) | copy-start | bytes 13828
  16.0 8.5 %copy-start.28 = (bf16[6,6,256]{2,1,0:T(8,128)(2,1)}, bf16[6,6,256]{2,1,0:T(8,128)(2,1)S(1)}, u32[]{:S(2)}) copy-start(bf16[6,6,256]{2,1,0:T(8,128)(2,1)S(1)} %bitcast_multiply_fusion.6) | copy-start | bytes 55300
  16.8 7.6 %copy-start.33 = (bf16[1,6,6,256]{3,2,1,0:T(8,128)(2,1)}, bf16[1,6,6,256]{3,2,1,0:T(8,128)(2,1)S(1)}, u32[]{:S(2)}) copy-start(bf16[1,6,6,256]{3,2,1,0:T(8,128)(2,1)S(1)} %broadcast_multiply_fusion.3) | copy-start | bytes 55300
  24.0 4.5 %copy-start.12 = (bf16[1,12,12,256]{3,2,1,0:T(8,128)(2,1)}, bf16[1,12,12,256]{3,2,1,0:T(8,128)(2,1)S(1)}, u32[]{:S(2)}) copy-start(bf16[1,12,12,256]{3,2,1,0:T(8,128)(2,1)S(1)} %broadcast_multiply_fusion.2) | copy-start | bytes 221188
  24.6 3.2 %copy-start.2 = (bf16[1,24,24,256]{3,2,1,0:T(8,128)(2,1)S(1)}, bf16[1,24,24,256]{3,2,1,0:T(8,128)(2,1)}, u32[]{:S(2)}) copy-start(bf16[1,24,24,256]{3,2,1,0:T(8,128)(2,1)} %param.13) | copy-start | bytes 884740
  29.9 2.3 copy-start.124
  29.9 2.3 copy-start.125
  32.2 45.2 %copy-start.45 = (f32[1,256]{1,0:T(1,128)}, f32[1,256]{1,0:T(1,128)S(1)}, u32[]{:S(2)}) copy-start(f32[1,256]{1,0:T(1,128)S(1)} %get-tuple-element.118) | copy-start | bytes 3076
  32.2 45.6 %copy-start.66 = (f32[1,256]{1,0:T(1,128)}, f32[1,256]{1,0:T(1,128)S(1)}, u32[]{:S(2)}) copy-start(f32[1,256]{1,0:T(1,128)S(1)} %get-tuple-element.117) | copy-start | bytes 3076
  32.2 45.7 %copy-start.69 = (f32[1,256]{1,0:T(1,128)}, f32[1,256]{1,0:T(1,128)S(1)}, u32[]{:S(2)}) copy-start(f32[1,256]{1,0:T(1,128)S(1)} %get-tuple-element.119) | copy-start | bytes 3076
  32.2 45.9 %copy-start.98 = (f32[1,256]{1,0:T(1,128)}, f32[1,256]{1,0:T(1,128)S(1)}, u32[]{:S(2)}) copy-start(f32[1,256]{1,0:T(1,128)S(1)} %get-tuple-element.116) | copy-start | bytes 3076
  32.3 45.1 %copy-start.56 = (f32[1,256]{1,0:T(1,128)}, f32[1,256]{1,0:T(1,128)S(1)}, u32[]{:S(2)}) copy-start(f32[1,256]{1,0:T(1,128)S(1)} %get-tuple-element.130) | copy-start | bytes 3076
  32.3 45.5 %copy-start.84 = (f32[1,256]{1,0:T(1,128)}, f32[1,256]{1,0:T(1,128)S(1)}, u32[]{:S(2)}) copy-start(f32[1,256]{1,0:T(1,128)S(1)} %get-tuple-element.129) | copy-start | bytes 3076
  32.3 45.7 %copy-start.87 = (f32[1,256]{1,0:T(1,128)}, f32[1,256]{1,0:T(1,128)S(1)}, u32[]{:S(2)}) copy-start(f32[1,256]{1,0:T(1,128)S(1)} %get-tuple-element.131) | copy-start | bytes 3076
  32.3 45.8 %copy-start.100 = (f32[1,256]{1,0:T(1,128)}, f32[1,256]{1,0:T(1,128)S(1)}, u32[]{:S(2)}) copy-start(f32[1,256]{1,0:T(1,128)S(1)} %get-tuple-element.128) | copy-start | bytes 3076
  34.5 3.6 %copy-start.118 = (f32[256]{0:T(256)S(1)}, f32[256]{0:T(256)}, u32[]{:S(2)}) copy-start(f32[256]{0:T(256)} %get-tuple-element.23) | copy-start | bytes 3076
  34.5 3.6 %copy-start.120 = (f32[256]{0:T(256)S(1)}, f32[256]{0:T(256)}, u32[]{:S(2)}) copy-start(f32[256]{0:T(256)} %get-tuple-element.21) | copy-start | bytes 3076
  34.5 3.6 %copy-start.117 = (f32[256]{0:T(256)S(1)}, f32[256]{0:T(256)}, u32[]{:S(2)}) copy-start(f32[256]{0:T(256)} %get-tuple-element.24) | copy-start | bytes 3076
  34.5 3.6 %copy-start.119 = (f32[256]{0:T(256)S(1)}, f32[256]{0:T(256)}, u32[]{:S(2)}) copy-start(f32[256]{0:T(256)} %get-tuple-element.22) | copy-start | bytes 3076
  34.6 42.8 %copy-start.1 = (bf16[1,24,24,256]{3,2,1,0:T(8,128)(2,1)S(1)}, bf16[1,24,24,256]{3,2,1,0:T(8,128)(2,1)}, u32[]{:S(2)}) copy-start(bf16[1,24,24,256]{3,2,1,0:T(8,128)(2,1)} %param.17) | copy-start | bytes 884740
  34.6 42.8 %copy-start.18 = (f32[24,24]{1,0:T(8,128)S(1)}, f32[24,24]{1,0:T(8,128)}, u32[]{:S(2)}) copy-start(f32[24,24]{1,0:T(8,128)} %get-tuple-element.150) | copy-start | bytes 6916
  35.2 42.6 %copy-start.7 = (bf16[1,12,12,256]{3,2,1,0:T(8,128)(2,1)S(1)}, bf16[1,12,12,256]{3,2,1,0:T(8,128)(2,1)}, u32[]{:S(2)}) copy-start(bf16[1,12,12,256]{3,2,1,0:T(8,128)(2,1)} %param.18) | copy-start | bytes 221188
  35.2 42.8 %copy-start.16 = (bf16[1,6,6,256]{3,2,1,0:T(8,128)(2,1)S(1)}, bf16[1,6,6,256]{3,2,1,0:T(8,128)(2,1)}, u32[]{:S(2)}) copy-start(bf16[1,6,6,256]{3,2,1,0:T(8,128)(2,1)} %param.19) | copy-start | bytes 55300
  35.2 42.8 %copy-start.37 = (f32[6,6]{1,0:T(8,128)S(1)}, f32[6,6]{1,0:T(8,128)}, u32[]{:S(2)}) copy-start(f32[6,6]{1,0:T(8,128)} %get-tuple-element.146) | copy-start | bytes 436
  35.2 43.0 %copy-start.26 = (f32[3,3,256]{2,1,0:T(4,128)S(1)}, f32[3,3,256]{2,1,0:T(4,128)}, u32[]{:S(2)}) copy-start(f32[3,3,256]{2,1,0:T(4,128)} %reshape.1121) | copy-start | bytes 27652
  35.2 43.0 %copy-start.48 = (f32[3,3]{1,0:T(4,128)S(1)}, f32[3,3]{1,0:T(4,128)}, u32[]{:S(2)}) copy-start(f32[3,3]{1,0:T(4,128)} %get-tuple-element.144) | copy-start | bytes 112
  35.2 43.0 %copy-start.74 = (bf16[1,3,3,256]{3,2,1,0:T(4,128)(2,1)S(1)}, bf16[1,3,3,256]{3,2,1,0:T(4,128)(2,1)}, u32[]{:S(2)}) copy-start(bf16[1,3,3,256]{3,2,1,0:T(4,128)(2,1)} %param.20) | copy-start | bytes 13828
  75.0 32.8 %copy-start.42 = (f32[1,256]{1,0:T(1,128)}, f32[1,256]{1,0:T(1,128)S(1)}, u32[]{:S(2)}) copy-start(f32[1,256]{1,0:T(1,128)S(1)} %get-tuple-element.123) | copy-start | bytes 3076
  75.0 32.8 %copy-start.60 = (f32[1,256]{1,0:T(1,128)}, f32[1,256]{1,0:T(1,128)S(1)}, u32[]{:S(2)}) copy-start(f32[1,256]{1,0:T(1,128)S(1)} %get-tuple-element.122) | copy-start | bytes 3076
  75.0 32.8 %copy-start.63 = (f32[1,256]{1,0:T(1,128)}, f32[1,256]{1,0:T(1,128)S(1)}, u32[]{:S(2)}) copy-start(f32[1,256]{1,0:T(1,128)S(1)} %get-tuple-element.121) | copy-start | bytes 3076
  75.0 32.8 %copy-start.72 = (f32[1,256]{1,0:T(1,128)}, f32[1,256]{1,0:T(1,128)S(1)}, u32[]{:S(2)}) copy-start(f32[1,256]{1,0:T(1,128)S(1)} %get-tuple-element.120) | copy-start | bytes 3076
  75.6 32.2 %copy-start.81 = (f32[256]{0:T(256)}, f32[256]{0:T(256)S(1)}, u32[]{:S(2)}) copy-start(f32[256]{0:T(256)S(1)} %get-tuple-element.137) | copy-start | bytes 3076
  76.2 31.6 %copy-start.92 = (f32[256]{0:T(256)}, f32[256]{0:T(256)S(1)}, u32[]{:S(2)}) copy-start(f32[256]{0:T(256)S(1)} %get-tuple-element.135) | copy-start | bytes 3076
  76.8 31.1 %copy-start.78 = (f32[256]{0:T(256)}, f32[256]{0:T(256)S(1)}, u32[]{:S(2)}) copy-start(f32[256]{0:T(256)S(1)} %get-tuple-element.139) | copy-start | bytes 3076
  77.4 30.5 %copy-start.52 = (f32[256]{0:T(256)}, f32[256]{0:T(256)S(1)}, u32[]{:S(2)}) copy-start(f32[256]{0:T(256)S(1)} %get-tuple-element.141) | copy-start | bytes 3076
  102.4 5.5 %copy-start.94 = (f32[4,256]{1,0:T(4,128)}, f32[4,256]{1,0:T(4,128)S(1)}, u32[]{:S(2)}) copy-start(f32[4,256]{1,0:T(4,128)S(1)} %get-tuple-element.28) | copy-start | bytes 12292
  102.4 5.5 %copy-start.96 = (f32[4,256]{1,0:T(4,128)}, f32[4,256]{1,0:T(4,128)S(1)}, u32[]{:S(2)}) copy-start(f32[4,256]{1,0:T(4,128)S(1)} %get-tuple-element.27) | copy-start | bytes 12292
  105.0 5.3 %copy-start.104 = (f32[1,256]{1,0:T(1,128)}, f32[1,256]{1,0:T(1,128)S(1)}, u32[]{:S(2)}) copy-start(f32[1,256]{1,0:T(1,128)S(1)} %get-tuple-element.113) | copy-start | bytes 3076
  105.0 9.1 %copy-start.115 = (f32[1,256]{1,0:T(1,128)}, f32[1,256]{1,0:T(1,128)S(1)}, u32[]{:S(2)}) copy-start(f32[1,256]{1,0:T(1,128)S(1)} %get-tuple-element.111) | copy-start | bytes 3076
  105.1 11.6 %copy-start.122 = (f32[1,256]{1,0:T(1,128)}, f32[1,256]{1,0:T(1,128)S(1)}, u32[]{:S(2)}) copy-start(f32[1,256]{1,0:T(1,128)S(1)} %get-tuple-element.110) | copy-start | bytes 3076
  105.1 14.1 %copy-start.111 = (f32[1,256]{1,0:T(1,128)}, f32[1,256]{1,0:T(1,128)S(1)}, u32[]{:S(2)}) copy-start(f32[1,256]{1,0:T(1,128)S(1)} %get-tuple-element.112) | copy-start | bytes 3076
  107.7 2.6 copy-start.106
  107.7 6.4 %copy-start.116 = (f32[1,256]{1,0:T(1,128)}, f32[1,256]{1,0:T(1,128)S(1)}, u32[]{:S(2)}) copy-start(f32[1,256]{1,0:T(1,128)S(1)} %get-tuple-element.107) | copy-start | bytes 3076
  107.7 9.0 %copy-start.123 = (f32[1,256]{1,0:T(1,128)}, f32[1,256]{1,0:T(1,128)S(1)}, u32[]{:S(2)}) copy-start(f32[1,256]{1,0:T(1,128)S(1)} %get-tuple-element.106) | copy-start | bytes 3076
  107.7 11.4 %copy-start.113 = (f32[1,256]{1,0:T(1,128)}, f32[1,256]{1,0:T(1,128)S(1)}, u32[]{:S(2)}) copy-start(f32[1,256]{1,0:T(1,128)S(1)} %get-tuple-element.108) | copy-start | bytes 3076
  118.2 2.5 copy-start.10
  123.0 3.9 %copy-start.11 = (bf16[12,12,256]{2,1,0:T(8,128)(2,1)S(1)}, bf16[12,12,256]{2,1,0:T(8,128)(2,1)}, u32[]{:S(2)}) copy-start(bf16[12,12,256]{2,1,0:T(8,128)(2,1)} %copy-done.10) | copy-start | bytes 221188
  123.0 14.6 %copy-start.25 = (f32[9,256]{1,0:T(8,128)S(1)}, f32[9,256]{1,0:T(8,128)}, u32[]{:S(2)}) copy-start(f32[9,256]{1,0:T(8,128)} %copy-done.24) | copy-start | bytes 27652
  123.0 165.9 %all-reduce.17.cloned.1.call-start = ((), (), s32[]{:S(2)}) async-start(), calls=%async_computation.1 | async-start | bytes 4718592 | tf_op jit(solution)/shard_map/psum | solution.py:88
  126.9 14.5 %copy-start.32 = (bf16[6,6,256]{2,1,0:T(8,128)(2,1)S(1)}, bf16[6,6,256]{2,1,0:T(8,128)(2,1)}, u32[]{:S(2)}) copy-start(bf16[6,6,256]{2,1,0:T(8,128)(2,1)} %get-tuple-element.70) | copy-start | bytes 55300
  126.9 14.5 %copy-start.31 = (bf16[6,6,256]{2,1,0:T(8,128)(2,1)S(1)}, bf16[6,6,256]{2,1,0:T(8,128)(2,1)}, u32[]{:S(2)}) copy-start(bf16[6,6,256]{2,1,0:T(8,128)(2,1)} %get-tuple-element.71) | copy-start | bytes 55300
  127.0 15.2 %copy-start.30 = (bf16[6,6,256]{2,1,0:T(8,128)(2,1)S(1)}, bf16[6,6,256]{2,1,0:T(8,128)(2,1)}, u32[]{:S(2)}) copy-start(bf16[6,6,256]{2,1,0:T(8,128)(2,1)} %get-tuple-element.72) | copy-start | bytes 55300
  134.8 4.8 %copy-start.51 = (bf16[9,256]{1,0:T(8,128)(2,1)S(1)}, bf16[9,256]{1,0:T(8,128)(2,1)}, u32[]{:S(2)}) copy-start(bf16[9,256]{1,0:T(8,128)(2,1)} %reshape.1155) | copy-start | bytes 13828
  134.8 5.0 %copy-start.50 = (bf16[9,256]{1,0:T(8,128)(2,1)S(1)}, bf16[9,256]{1,0:T(8,128)(2,1)}, u32[]{:S(2)}) copy-start(bf16[9,256]{1,0:T(8,128)(2,1)} %reshape.1156) | copy-start | bytes 13828
  144.8 3.3 %copy-start.15 = (f32[36,256]{1,0:T(8,128)S(1)}, f32[36,256]{1,0:T(8,128)}, u32[]{:S(2)}) copy-start(f32[36,256]{1,0:T(8,128)} %copy-done.14) | copy-start | bytes 110596
  144.8 3.3 %copy-start.65 = (f32[1,256]{1,0:T(1,128)S(1)}, f32[1,256]{1,0:T(1,128)}, u32[]{:S(2)}) copy-start(f32[1,256]{1,0:T(1,128)} %copy-done.63) | copy-start | bytes 3076
  144.8 3.3 %copy-start.71 = (f32[1,256]{1,0:T(1,128)S(1)}, f32[1,256]{1,0:T(1,128)}, u32[]{:S(2)}) copy-start(f32[1,256]{1,0:T(1,128)} %copy-done.69) | copy-start | bytes 3076
  144.8 3.3 %copy-start.83 = (f32[256]{0:T(256)S(1)}, f32[256]{0:T(256)}, u32[]{:S(2)}) copy-start(f32[256]{0:T(256)} %copy-done.81) | copy-start | bytes 3076
  144.8 3.3 %copy-start.89 = (f32[1,256]{1,0:T(1,128)S(1)}, f32[1,256]{1,0:T(1,128)}, u32[]{:S(2)}) copy-start(f32[1,256]{1,0:T(1,128)} %copy-done.87) | copy-start | bytes 3076
  144.9 4.2 %copy-start.36 = (bf16[36,256]{1,0:T(8,128)(2,1)S(1)}, bf16[36,256]{1,0:T(8,128)(2,1)}, u32[]{:S(2)}) copy-start(bf16[36,256]{1,0:T(8,128)(2,1)} %reshape.1144) | copy-start | bytes 55300
  145.0 4.4 %copy-start.35 = (bf16[36,256]{1,0:T(8,128)(2,1)S(1)}, bf16[36,256]{1,0:T(8,128)(2,1)}, u32[]{:S(2)}) copy-start(bf16[36,256]{1,0:T(8,128)(2,1)} %reshape.1145) | copy-start | bytes 55300
  (65 other events, 87.7 us)
Sparse Core Ops, SparseCore 0:
  123.2 53.5 all-reduce.14
  180.3 108.6 all-reduce.16
where the time goes:
time: 301 us; the launch traced here: 299 us
  waiting for transfers between devices  127 us (42%)
  blocking collectives  54.4 us (18%)
  other arithmetic  41.2 us (14%)
  matrix products  34 us (11%)
  local copies, waits for them, and re-layouts  24.6 us (8%)
  between operations  18.1 us (6%)
    psum x1, waiting for transfers between devices, combine_grads(): result = lax.psum(within, 'wide')  106 us
    psum x2, blocking collectives, combine_stats(): result = lax.psum(within, 'wide')  39.7 us
    psum x1, waiting for transfers between devices, combine_grads(): within = lax.psum(values, 'group')  20.6 us
    psum x2, blocking collectives, combine_stats(): within = lax.psum(values, 'group')  14.6 us
    dot_general x36, matrix products, input_grad_rows(): lax.dot_general(window.reshape(row_count * extent, -1), conv_weight[tap_r...  14.1 us
    reshape x24, local copies, waits for them, and re-layouts, input_grad_rows(): window.reshape(row_count * extent, -1)  11.1 us
    dot_general x36, matrix products, conv_rows(): jnp.dot(window.reshape(row_count * extent, -1), conv_weight[tap_row, tap_...  10.4 us
    dot_general x36, matrix products, weight_grad_rows(): lax.dot_general(window.reshape(row_count * extent, -1), flat_back, (((0,)...  9.51 us
  transfers between devices with their start and end apart: 2, of which 2 were waited for; matrix products, arithmetic and copies ran while one was open for 12% of the time, Pallas kernels for 0%

commit v1 on v0

--- a/solution.py
+++ b/solution.py
@@ -84,7 +84,7 @@
 
 
 def combine_grads(values):
-    within = lax.psum(values, "group")
+    within = jnp.sum(lax.all_gather(values, "group"), axis=0)
     result = lax.psum(within, "wide")
     return result
 

time: 301 us -> 311 us (1.033)
  waiting for transfers between devices: 127 us -> 150 us
  local copies, waits for them, and re-layouts: 24.6 us -> 12.8 us
  matrix products: 34 us -> 28.4 us
  other arithmetic: 41.2 us -> 45.6 us
    all_gather x0 -> x1, waiting for transfers between devices: none -> 47.6 us  [combine_grads(): within = jnp.sum(lax.all_gather(values, 'group'), axis=0)]
    psum x1 -> x0, waiting for transfers between devices: 20.6 us -> none  [combine_grads(): within = lax.psum(values, 'group')]
    reshape x24, local copies, waits for them, and re-layouts: 11.1 us -> 0.41 us  [input_grad_rows(): window.reshape(row_count * extent, -1)]
    reduce_sum x0 -> x1, other arithmetic: none -> 6.04 us  [combine_grads(): within = jnp.sum(lax.all_gather(values, 'group'), axis=0)]
    dot_general x36, matrix products: 14.1 us -> 8.52 us  [input_grad_rows(): lax.dot_general(window.reshape(row_count * extent, -1), conv_weight[tap_r...]
    psum x1, waiting for transfers between devices: 106 us -> 102 us  [combine_grads(): result = lax.psum(within, 'wide')]
  transfers between devices with their start and end apart: 2 -> 2, of which waited for: 2 -> 2; matrix products, arithmetic and copies ran while one was open for 12% -> 6% of each run, Pallas kernels for 0% -> 0%
where the time goes in v1:
time: 311 us; the launch traced here: 310 us
  waiting for transfers between devices  150 us (48%)
  blocking collectives  54.4 us (17%)
  other arithmetic  45.6 us (15%)
  matrix products  28.4 us (9%)
  between operations  18.1 us (6%)
  local copies, waits for them, and re-layouts  12.8 us (4%)
    psum x1, waiting for transfers between devices, combine_grads(): result = lax.psum(within, 'wide')  102 us
    all_gather x1, waiting for transfers between devices, combine_grads(): within = jnp.sum(lax.all_gather(values, 'group'), axis=0)  47.6 us
    psum x2, blocking collectives, combine_stats(): result = lax.psum(within, 'wide')  39.7 us
    psum x2, blocking collectives, combine_stats(): within = lax.psum(values, 'group')  14.8 us
    dot_general x36, matrix products, conv_rows(): jnp.dot(window.reshape(row_count * extent, -1), conv_weight[tap_row, tap_...  10.4 us
    dot_general x36, matrix products, weight_grad_rows(): lax.dot_general(window.reshape(row_count * extent, -1), flat_back, (((0,)...  9.51 us
    dot_general x36, matrix products, input_grad_rows(): lax.dot_general(window.reshape(row_count * extent, -1), conv_weight[tap_r...  8.52 us
  transfers between devices with their start and end apart: 2, of which 2 were waited for; matrix products, arithmetic and copies ran while one was open for 6% of the time, Pallas kernels for 0%

profile of v1, /device:TPU:0, one launch (start us, length us, event | category | flops | bytes accessed | tf_op | source)
XLA Modules:
  0.0 309.5 jit_solution(1283323995085464418)
XLA Ops:
  8.7 0.7 fusion.283
  9.4 0.6 and_convert_fusion.9
  10.0 0.7 fusion.281
  10.8 0.7 and_convert_fusion.3
  11.4 0.8 bitcast_multiply_fusion.8
  12.2 0.8 broadcast_multiply_fusion.4
  13.0 0.7 fusion.268
  13.7 0.7 fusion.257
  14.4 0.7 and_convert_fusion
  15.1 0.8 bitcast_multiply_fusion.6
  15.9 0.8 broadcast_multiply_fusion.3
  17.3 1.0 fusion.131
  18.3 1.1 convolution_add_fusion.63
  19.4 1.1 convolution_add_fusion.62
  21.2 0.6 and_convert_fusion.5
  21.8 0.7 multiply_reduce_fusion.6
  22.5 0.6 reshape.1154
  23.2 0.6 reshape.1158
  25.8 0.6 and_convert_fusion.6
  26.4 0.7 multiply_reduce_fusion.4
  27.1 0.6 reshape.1153
  30.2 0.6 and_convert_fusion.7
  31.0 0.7 reshape.1152
  34.6 0.6 and_convert_fusion.2
  35.5 2.4 pad_maximum_fusion.4
  38.0 8.8 %all-reduce.11 = (f32[4,256]{1,0:T(4,128)S(1)}, f32[4]{0:T(128)S(1)}, f32[4,256]{1,0:T(4,128)S(1)}) all-reduce(f32[4,256]{1,0:T(4,128)S(1)} %pad_maximum_fusion.1, f32[4]{0:T(128)S(1)} %pad_maximum_fusion.4, f32[4,256]{1,0:T(4,128)S(1)} %pad_maximum_fusion), channel_id=1, replica_groups=mesh['wide'=8,'group'=4] {'group'}, use_global_device_ids=true, to_apply=%region_16.17 | all-reduce | flops 2052 | bytes 16416 | tf_op jit(solution)/shard_map/psum | solution.py:81
  46.7 22.1 %all-reduce.9 = (f32[4,256]{1,0:T(4,128)S(1)}, f32[4]{0:T(128)S(1)}, f32[4,256]{1,0:T(4,128)S(1)}) all-reduce(f32[4,256]{1,0:T(4,128)S(1)} %get-tuple-element.34, f32[4]{0:T(128)S(1)} %get-tuple-element.35, f32[4,256]{1,0:T(4,128)S(1)} %get-tuple-element.36), channel_id=1, replica_groups=mesh['wide'=8,'group'=4] {'wide'}, use_global_device_ids=true, to_apply=%region_17.18 | all-reduce | flops 2052 | bytes 16416 | tf_op jit(solution)/shard_map/psum | solution.py:82
  68.9 0.7 fusion.303
  69.5 2.5 slice_divide_fusion.8
  72.0 2.5 slice_divide_fusion.9
  74.6 0.6 fusion.286
  75.2 0.6 fusion.285
  75.7 0.6 fusion.287
  76.3 0.5 fusion.288
  76.9 0.4 fusion.298
  77.7 0.7 fusion.299
  78.4 6.0 %all-reduce.10 = (f32[4,256]{1,0:T(4,128)S(1)}, f32[4,256]{1,0:T(4,128)S(1)}) all-reduce(f32[4,256]{1,0:T(4,128)S(1)} %pad_maximum_fusion.3, f32[4,256]{1,0:T(4,128)S(1)} %pad_maximum_fusion.2), channel_id=1, replica_groups=mesh['wide'=8,'group'=4] {'group'}, use_global_device_ids=true, to_apply=%region_28.29 | all-reduce | flops 2048 | bytes 16384 | tf_op jit(solution)/shard_map/psum | solution.py:81
  84.4 17.6 %all-reduce.8 = (f32[4,256]{1,0:T(4,128)S(1)}, f32[4,256]{1,0:T(4,128)S(1)}) all-reduce(f32[4,256]{1,0:T(4,128)S(1)} %get-tuple-element.32, f32[4,256]{1,0:T(4,128)S(1)} %get-tuple-element.33), channel_id=1, replica_groups=mesh['wide'=8,'group'=4] {'wide'}, use_global_device_ids=true, to_apply=%region_29.30 | all-reduce | flops 2048 | bytes 16384 | tf_op jit(solution)/shard_map/psum | solution.py:82
  102.0 2.5 slice_divide_fusion
  104.5 2.5 slice_divide_fusion.1
  107.1 1.1 multiply_convert_fusion.2
  110.0 0.6 fusion.4
  112.0 0.3 copy-done.15
  118.5 0.4 copy-done.8
  120.2 2.1 add_add_fusion
  122.7 0.7 reshape.1200
  125.2 0.6 reshape.1194
  129.1 1.2 convolution_add_fusion.20
  131.1 0.7 reshape.1176
  131.9 1.2 pad_slice_fusion
  133.2 0.6 broadcast_multiply_fusion.6
  133.8 0.6 broadcast_multiply_fusion.5
  134.5 0.7 multiply_convert_fusion.21
  135.2 0.7 multiply_convert_fusion.13
  136.2 0.4 fusion.42
  136.9 47.6 %all-gather.2.cloned.1.call-done = f32[4,3,3,256,256]{4,3,2,1,0:T(8,128)} async-done(((f32[1,3,3,256,256]{4,3,2,1,0:T(8,128)}), f32[4,3,3,256,256]{4,3,2,1,0:T(8,128)}) %all-gather.2.cloned.1.call-update) | async-done | bytes 9437200 | tf_op jit(solution)/shard_map/all_gather | solution.py:87
  184.6 6.0 %reduce_sum.209 = f32[3,3,256,256]{3,2,1,0:T(8,128)} reduce(f32[4,3,3,256,256]{4,3,2,1,0:T(8,128)} %all-gather.2.cloned.1.call-done, f32[]{:T(128)} %constant.111.clone.1), dimensions={0}, to_apply=%region_30.31 | reduce | flops 1769472 | bytes 11796484 | tf_op jit(solution)/shard_map/reduce_sum | solution.py:87
  190.7 0.6 copy-done.56
  191.2 1.8 multiply_convert_fusion.6
  193.9 0.7 copy-done.4
  195.8 0.4 copy-done.18
  196.2 1.1 multiply_convert_fusion.1
  197.2 102.2 %all-reduce.14.cloned.1.call-done = f32[3,3,256,256]{3,2,1,0:T(8,128)} async-done(((f32[3,3,256,256]{3,2,1,0:T(8,128)}), f32[3,3,256,256]{3,2,1,0:T(8,128)}) %all-reduce.14.cloned.1.call-update) | async-done | bytes 2359312 | tf_op jit(solution)/shard_map/psum | solution.py:88
  299.4 3.3 %broadcast_multiply_fusion = f32[3,3,256,256]{3,2,1,0:T(8,128)} fusion(f32[3,3,256,256]{3,2,1,0:T(8,128)} %all-reduce.14.cloned.1.call-done), kind=kLoop, calls=%fused_computation.17 | loop fusion | flops 589824 | bytes 4718592 | tf_op jit(solution)/shard_map/div | solution.py:191
  (465 shorter events, 27.4 us)
Async XLA Ops:
  7.2 13.3 %copy-start = (bf16[3,3,256,256]{3,2,1,0:T(8,128)(2,1)S(1)}, bf16[3,3,256,256]{3,2,1,0:T(8,128)(2,1)}, u32[]{:S(2)}) copy-start(bf16[3,3,256,256]{3,2,1,0:T(8,128)(2,1)} %param.21) | copy-start | bytes 3538948
  7.2 16.6 %copy-start.9 = (bf16[1,12,12,256]{3,2,1,0:T(8,128)(2,1)S(1)}, bf16[1,12,12,256]{3,2,1,0:T(8,128)(2,1)}, u32[]{:S(2)}) copy-start(bf16[1,12,12,256]{3,2,1,0:T(8,128)(2,1)} %param.14) | copy-start | bytes 221188
  7.2 177.4 %all-gather.2.cloned.1.call-start = ((), (), s32[]{:S(2)}) async-start(), calls=%async_computation | async-start | bytes 11796480 | tf_op jit(solution)/shard_map/all_gather | solution.py:87
  13.0 4.1 %copy-start.70 = (bf16[1,3,3,256]{3,2,1,0:T(4,128)(2,1)}, bf16[1,3,3,256]{3,2,1,0:T(4,128)(2,1)S(1)}, u32[]{:S(2)}) copy-start(bf16[1,3,3,256]{3,2,1,0:T(4,128)(2,1)S(1)} %broadcast_multiply_fusion.4) | copy-start | bytes 13828
  15.9 8.5 %copy-start.25 = (bf16[6,6,256]{2,1,0:T(8,128)(2,1)}, bf16[6,6,256]{2,1,0:T(8,128)(2,1)S(1)}, u32[]{:S(2)}) copy-start(bf16[6,6,256]{2,1,0:T(8,128)(2,1)S(1)} %bitcast_multiply_fusion.6) | copy-start | bytes 55300
  16.7 7.6 %copy-start.27 = (bf16[1,6,6,256]{3,2,1,0:T(8,128)(2,1)}, bf16[1,6,6,256]{3,2,1,0:T(8,128)(2,1)S(1)}, u32[]{:S(2)}) copy-start(bf16[1,6,6,256]{3,2,1,0:T(8,128)(2,1)S(1)} %broadcast_multiply_fusion.3) | copy-start | bytes 55300
  24.0 4.5 %copy-start.10 = (bf16[1,12,12,256]{3,2,1,0:T(8,128)(2,1)}, bf16[1,12,12,256]{3,2,1,0:T(8,128)(2,1)S(1)}, u32[]{:S(2)}) copy-start(bf16[1,12,12,256]{3,2,1,0:T(8,128)(2,1)S(1)} %broadcast_multiply_fusion.2) | copy-start | bytes 221188
  24.5 3.2 %copy-start.2 = (bf16[1,24,24,256]{3,2,1,0:T(8,128)(2,1)S(1)}, bf16[1,24,24,256]{3,2,1,0:T(8,128)(2,1)}, u32[]{:S(2)}) copy-start(bf16[1,24,24,256]{3,2,1,0:T(8,128)(2,1)} %param.13) | copy-start | bytes 884740
  32.2 44.7 %copy-start.39 = (f32[1,256]{1,0:T(1,128)}, f32[1,256]{1,0:T(1,128)S(1)}, u32[]{:S(2)}) copy-start(f32[1,256]{1,0:T(1,128)S(1)} %get-tuple-element.118) | copy-start | bytes 3076
  32.2 45.1 %copy-start.60 = (f32[1,256]{1,0:T(1,128)}, f32[1,256]{1,0:T(1,128)S(1)}, u32[]{:S(2)}) copy-start(f32[1,256]{1,0:T(1,128)S(1)} %get-tuple-element.117) | copy-start | bytes 3076
  32.2 45.3 %copy-start.62 = (f32[1,256]{1,0:T(1,128)}, f32[1,256]{1,0:T(1,128)S(1)}, u32[]{:S(2)}) copy-start(f32[1,256]{1,0:T(1,128)S(1)} %get-tuple-element.119) | copy-start | bytes 3076
  32.2 45.4 %copy-start.92 = (f32[1,256]{1,0:T(1,128)}, f32[1,256]{1,0:T(1,128)S(1)}, u32[]{:S(2)}) copy-start(f32[1,256]{1,0:T(1,128)S(1)} %get-tuple-element.116) | copy-start | bytes 3076
  32.2 44.6 %copy-start.50 = (f32[1,256]{1,0:T(1,128)}, f32[1,256]{1,0:T(1,128)S(1)}, u32[]{:S(2)}) copy-start(f32[1,256]{1,0:T(1,128)S(1)} %get-tuple-element.130) | copy-start | bytes 3076
  32.2 45.0 %copy-start.78 = (f32[1,256]{1,0:T(1,128)}, f32[1,256]{1,0:T(1,128)S(1)}, u32[]{:S(2)}) copy-start(f32[1,256]{1,0:T(1,128)S(1)} %get-tuple-element.129) | copy-start | bytes 3076
  32.3 45.2 %copy-start.81 = (f32[1,256]{1,0:T(1,128)}, f32[1,256]{1,0:T(1,128)S(1)}, u32[]{:S(2)}) copy-start(f32[1,256]{1,0:T(1,128)S(1)} %get-tuple-element.131) | copy-start | bytes 3076
  32.3 45.3 %copy-start.95 = (f32[1,256]{1,0:T(1,128)}, f32[1,256]{1,0:T(1,128)S(1)}, u32[]{:S(2)}) copy-start(f32[1,256]{1,0:T(1,128)S(1)} %get-tuple-element.128) | copy-start | bytes 3076
  34.5 3.4 %copy-start.116 = (f32[256]{0:T(256)S(1)}, f32[256]{0:T(256)}, u32[]{:S(2)}) copy-start(f32[256]{0:T(256)} %get-tuple-element.23) | copy-start | bytes 3076
  34.5 3.4 %copy-start.118 = (f32[256]{0:T(256)S(1)}, f32[256]{0:T(256)}, u32[]{:S(2)}) copy-start(f32[256]{0:T(256)} %get-tuple-element.21) | copy-start | bytes 3076
  34.5 3.4 %copy-start.115 = (f32[256]{0:T(256)S(1)}, f32[256]{0:T(256)}, u32[]{:S(2)}) copy-start(f32[256]{0:T(256)} %get-tuple-element.24) | copy-start | bytes 3076
  34.5 3.4 %copy-start.117 = (f32[256]{0:T(256)S(1)}, f32[256]{0:T(256)}, u32[]{:S(2)}) copy-start(f32[256]{0:T(256)} %get-tuple-element.22) | copy-start | bytes 3076
  34.5 42.3 %copy-start.1 = (bf16[1,24,24,256]{3,2,1,0:T(8,128)(2,1)S(1)}, bf16[1,24,24,256]{3,2,1,0:T(8,128)(2,1)}, u32[]{:S(2)}) copy-start(bf16[1,24,24,256]{3,2,1,0:T(8,128)(2,1)} %param.17) | copy-start | bytes 884740
  34.5 42.3 %copy-start.16 = (f32[24,24]{1,0:T(8,128)S(1)}, f32[24,24]{1,0:T(8,128)}, u32[]{:S(2)}) copy-start(f32[24,24]{1,0:T(8,128)} %get-tuple-element.150) | copy-start | bytes 6916
  35.2 42.1 %copy-start.7 = (bf16[1,12,12,256]{3,2,1,0:T(8,128)(2,1)S(1)}, bf16[1,12,12,256]{3,2,1,0:T(8,128)(2,1)}, u32[]{:S(2)}) copy-start(bf16[1,12,12,256]{3,2,1,0:T(8,128)(2,1)} %param.18) | copy-start | bytes 221188
  35.2 42.3 %copy-start.14 = (bf16[1,6,6,256]{3,2,1,0:T(8,128)(2,1)S(1)}, bf16[1,6,6,256]{3,2,1,0:T(8,128)(2,1)}, u32[]{:S(2)}) copy-start(bf16[1,6,6,256]{3,2,1,0:T(8,128)(2,1)} %param.19) | copy-start | bytes 55300
  35.2 42.3 %copy-start.29 = (f32[6,6]{1,0:T(8,128)S(1)}, f32[6,6]{1,0:T(8,128)}, u32[]{:S(2)}) copy-start(f32[6,6]{1,0:T(8,128)} %get-tuple-element.146) | copy-start | bytes 436
  35.2 42.5 %copy-start.23 = (f32[3,3,256]{2,1,0:T(4,128)S(1)}, f32[3,3,256]{2,1,0:T(4,128)}, u32[]{:S(2)}) copy-start(f32[3,3,256]{2,1,0:T(4,128)} %reshape.1158) | copy-start | bytes 27652
  35.2 42.5 %copy-start.43 = (f32[3,3]{1,0:T(4,128)S(1)}, f32[3,3]{1,0:T(4,128)}, u32[]{:S(2)}) copy-start(f32[3,3]{1,0:T(4,128)} %get-tuple-element.144) | copy-start | bytes 112
  35.2 42.5 %copy-start.68 = (bf16[1,3,3,256]{3,2,1,0:T(4,128)(2,1)S(1)}, bf16[1,3,3,256]{3,2,1,0:T(4,128)(2,1)}, u32[]{:S(2)}) copy-start(bf16[1,3,3,256]{3,2,1,0:T(4,128)(2,1)} %param.20) | copy-start | bytes 13828
  74.5 32.5 %copy-start.36 = (f32[1,256]{1,0:T(1,128)}, f32[1,256]{1,0:T(1,128)S(1)}, u32[]{:S(2)}) copy-start(f32[1,256]{1,0:T(1,128)S(1)} %get-tuple-element.123) | copy-start | bytes 3076
  74.5 32.5 %copy-start.54 = (f32[1,256]{1,0:T(1,128)}, f32[1,256]{1,0:T(1,128)S(1)}, u32[]{:S(2)}) copy-start(f32[1,256]{1,0:T(1,128)S(1)} %get-tuple-element.122) | copy-start | bytes 3076
  74.6 32.5 %copy-start.57 = (f32[1,256]{1,0:T(1,128)}, f32[1,256]{1,0:T(1,128)S(1)}, u32[]{:S(2)}) copy-start(f32[1,256]{1,0:T(1,128)S(1)} %get-tuple-element.121) | copy-start | bytes 3076
  74.6 32.5 %copy-start.65 = (f32[1,256]{1,0:T(1,128)}, f32[1,256]{1,0:T(1,128)S(1)}, u32[]{:S(2)}) copy-start(f32[1,256]{1,0:T(1,128)S(1)} %get-tuple-element.120) | copy-start | bytes 3076
  75.2 31.9 %copy-start.75 = (f32[256]{0:T(256)}, f32[256]{0:T(256)S(1)}, u32[]{:S(2)}) copy-start(f32[256]{0:T(256)S(1)} %get-tuple-element.137) | copy-start | bytes 3076
  75.7 31.4 %copy-start.85 = (f32[256]{0:T(256)}, f32[256]{0:T(256)S(1)}, u32[]{:S(2)}) copy-start(f32[256]{0:T(256)S(1)} %get-tuple-element.135) | copy-start | bytes 3076
  76.3 30.8 %copy-start.72 = (f32[256]{0:T(256)}, f32[256]{0:T(256)S(1)}, u32[]{:S(2)}) copy-start(f32[256]{0:T(256)S(1)} %get-tuple-element.139) | copy-start | bytes 3076
  76.9 30.3 %copy-start.46 = (f32[256]{0:T(256)}, f32[256]{0:T(256)S(1)}, u32[]{:S(2)}) copy-start(f32[256]{0:T(256)S(1)} %get-tuple-element.141) | copy-start | bytes 3076
  101.9 5.2 %copy-start.88 = (f32[4,256]{1,0:T(4,128)}, f32[4,256]{1,0:T(4,128)S(1)}, u32[]{:S(2)}) copy-start(f32[4,256]{1,0:T(4,128)S(1)} %get-tuple-element.28) | copy-start | bytes 12292
  102.0 5.2 %copy-start.90 = (f32[4,256]{1,0:T(4,128)}, f32[4,256]{1,0:T(4,128)S(1)}, u32[]{:S(2)}) copy-start(f32[4,256]{1,0:T(4,128)S(1)} %get-tuple-element.27) | copy-start | bytes 12292
  104.5 5.2 %copy-start.100 = (f32[1,256]{1,0:T(1,128)}, f32[1,256]{1,0:T(1,128)S(1)}, u32[]{:S(2)}) copy-start(f32[1,256]{1,0:T(1,128)S(1)} %get-tuple-element.113) | copy-start | bytes 3076
  104.5 9.0 %copy-start.111 = (f32[1,256]{1,0:T(1,128)}, f32[1,256]{1,0:T(1,128)S(1)}, u32[]{:S(2)}) copy-start(f32[1,256]{1,0:T(1,128)S(1)} %get-tuple-element.111) | copy-start | bytes 3076
  104.5 11.5 %copy-start.120 = (f32[1,256]{1,0:T(1,128)}, f32[1,256]{1,0:T(1,128)S(1)}, u32[]{:S(2)}) copy-start(f32[1,256]{1,0:T(1,128)S(1)} %get-tuple-element.110) | copy-start | bytes 3076
  104.5 14.0 %copy-start.107 = (f32[1,256]{1,0:T(1,128)}, f32[1,256]{1,0:T(1,128)S(1)}, u32[]{:S(2)}) copy-start(f32[1,256]{1,0:T(1,128)S(1)} %get-tuple-element.112) | copy-start | bytes 3076
  107.0 2.6 copy-start.102
  107.0 6.4 %copy-start.113 = (f32[1,256]{1,0:T(1,128)}, f32[1,256]{1,0:T(1,128)S(1)}, u32[]{:S(2)}) copy-start(f32[1,256]{1,0:T(1,128)S(1)} %get-tuple-element.107) | copy-start | bytes 3076
  107.0 9.0 %copy-start.122 = (f32[1,256]{1,0:T(1,128)}, f32[1,256]{1,0:T(1,128)S(1)}, u32[]{:S(2)}) copy-start(f32[1,256]{1,0:T(1,128)S(1)} %get-tuple-element.106) | copy-start | bytes 3076
  107.0 11.4 %copy-start.109 = (f32[1,256]{1,0:T(1,128)}, f32[1,256]{1,0:T(1,128)S(1)}, u32[]{:S(2)}) copy-start(f32[1,256]{1,0:T(1,128)S(1)} %get-tuple-element.108) | copy-start | bytes 3076
  122.4 177.1 %all-reduce.14.cloned.1.call-start = ((), (), s32[]{:S(2)}) async-start(), calls=%async_computation.1 | async-start | bytes 4718592 | tf_op jit(solution)/shard_map/psum | solution.py:88
  131.8 2.6 copy-start.33
  131.8 2.6 copy-start.34
  131.8 2.6 copy-start.45
  131.9 3.3 %copy-start.20 = (f32[1,6,6,256]{3,2,1,0:T(8,128)S(1)}, f32[1,6,6,256]{3,2,1,0:T(8,128)}, u32[]{:S(2)}) copy-start(f32[1,6,6,256]{3,2,1,0:T(8,128)} %reshape.1153) | copy-start | bytes 110596
  131.9 3.3 %copy-start.31 = (f32[6,6]{1,0:T(8,128)S(1)}, f32[6,6]{1,0:T(8,128)}, u32[]{:S(2)}) copy-start(f32[6,6]{1,0:T(8,128)} %get-tuple-element.146) | copy-start | bytes 436
  131.9 3.3 %copy-start.59 = (f32[1,256]{1,0:T(1,128)S(1)}, f32[1,256]{1,0:T(1,128)}, u32[]{:S(2)}) copy-start(f32[1,256]{1,0:T(1,128)} %copy-done.57) | copy-start | bytes 3076
  131.9 3.2 %copy-start.64 = (f32[1,256]{1,0:T(1,128)S(1)}, f32[1,256]{1,0:T(1,128)}, u32[]{:S(2)}) copy-start(f32[1,256]{1,0:T(1,128)} %copy-done.62) | copy-start | bytes 3076
  131.9 3.2 %copy-start.77 = (f32[256]{0:T(256)S(1)}, f32[256]{0:T(256)}, u32[]{:S(2)}) copy-start(f32[256]{0:T(256)} %copy-done.75) | copy-start | bytes 3076
  131.9 3.2 %copy-start.83 = (f32[1,256]{1,0:T(1,128)S(1)}, f32[1,256]{1,0:T(1,128)}, u32[]{:S(2)}) copy-start(f32[1,256]{1,0:T(1,128)} %copy-done.81) | copy-start | bytes 3076
  133.2 3.0 copy-start.38
  133.2 3.0 copy-start.41
  133.2 3.0 copy-start.48
  133.2 3.0 copy-start.52
  133.2 3.0 copy-start.84
  133.2 3.0 copy-start.99
  133.2 3.0 copy-start.101
  133.2 3.0 copy-start.103
  (67 other events, 94.7 us)
Sparse Core Ops, SparseCore 0:
  122.4 62.1 all-gather.1
  190.8 108.5 all-reduce.13
